TPU v7x, 256 devices: a whole 4x4x8 slice. The times are simulated.
256 devices in a mesh: space: 64 (over z, y, core), tm: 4 (over x).
Axes of the slice: x: 4, y: 4, z: 8, core: 2. Of those that a mesh axis runs over, the one named last changes fastest.
Arguments:
- precip: float32 [512, 384, 2048], P('tm', 'space'), may hold values from 0.0001 to 0.01
Outputs:
- totals: float32 [384, 2048, 512], P(None, 'space', 'tm')
All inputs are finite; a program needn't handle non-finite values.
Results may differ from a plain program's by a relative error of at most 0.00005.
Values sent between devices are 32-bit elements; how exact they have to be, the bound alone decides.
No kernel may reach another device: no remote copies, remote signals or barrier semaphores. Data moves between devices by JAX's collectives and lax.ppermute only.
A program may use at most 64 MiB of HBM per device.

v0:
```python
import jax
import jax.numpy as jnp
from jax import lax
from jax.sharding import Mesh
from jax.sharding import PartitionSpec as P

SPACE = ("space_0", "space_1", "space_2")


def in_blocks(value, dim, peers):
    before, after = (value.shape[:dim], value.shape[dim + 1 :])
    return jnp.moveaxis(value.reshape(*before, peers, -1, *after), dim, 0)


def joined_along(pieces, dim):
    pieces = jnp.moveaxis(pieces, 0, dim)
    dims = pieces.shape
    return pieces.reshape(*dims[:dim], dims[dim] * dims[dim + 1], *dims[dim + 2 :])


def moved_by_axis(pieces, axes, order):
    dims = [lax.axis_size(a) for a in axes]
    pieces = pieces.reshape(*dims, *pieces.shape[1:])
    for k in order:
        pieces = lax.all_to_all(pieces, axes[k], split_axis=k, concat_axis=k, tiled=True)
    return pieces.reshape(-1, *pieces.shape[len(axes) :])


def core_and_chips(value, groups, order, split_dim, concat_dim):
    peers = lax.axis_size(groups[0]) * lax.axis_size(groups[1])
    pieces = in_blocks(value, split_dim, peers)
    return joined_along(moved_by_axis(pieces, groups, order), concat_dim)


def from_everyone(value, axis):
    copies = jnp.broadcast_to(value, (lax.axis_size(axis), *value.shape))
    return lax.all_to_all(copies, axis, split_axis=0, concat_axis=0, tiled=True)


def folded_in_pairs(pieces, combine):
    while len(jax.tree.leaves(pieces)[0]) > 1:
        pieces = jax.vmap(combine)(*(pieces[side::2] for side in (0, 1)))
    return pieces[0]


def carried_in(value, axis, combine, identity):
    peers, mine = (lax.axis_size(axis), lax.axis_index(axis))
    passed = jnp.arange(peers) < mine

    def kept(part, zero, own):
        part = jnp.where(
            passed.reshape(-1, *(1 for _ in own.shape)), part, jnp.asarray(zero, own.dtype)
        )
        return part

    pieces = from_everyone(value, axis)
    return folded_in_pairs(kept(pieces, identity, value), combine)


def rechunk(source):
    return core_and_chips(source, (("space_0", "space_1"), "space_2"), (1, 0), 2, 1)


def add_terms(earlier_part, later_part):
    return earlier_part + later_part


def per_device(precip):
    day_count = precip.shape[0]
    position = lax.broadcasted_iota(jnp.int32, (day_count, day_count), 0)
    later_pos = lax.broadcasted_iota(jnp.int32, (day_count, day_count), 1)
    upper_ones = (position <= later_pos).astype(jnp.float32)
    flat_days = precip.reshape(day_count, -1)
    running = jnp.dot(
        upper_ones.T, flat_days, precision=lax.Precision.HIGHEST, preferred_element_type=jnp.float32
    )
    running = running.reshape(precip.shape)
    last_day = running[-1]
    carried = carried_in(last_day, "tm", add_terms, jnp.zeros_like(last_day))
    return jnp.transpose(rechunk(running + carried[None]), (1, 2, 0))


def solution(mesh):
    finer = Mesh(
        mesh.devices.reshape(8, 4, 2, mesh.shape["tm"]), ("space_0", "space_1", "space_2", "tm")
    )
    placed = (P("tm", SPACE, None),)
    return jax.shard_map(
        per_device, mesh=finer, in_specs=placed, out_specs=P(None, SPACE, "tm"), check_vma=False
    )
```

profile of v0, /device:TPU:10, one launch (start us, length us, event | category | flops | bytes accessed | tf_op | source)
XLA Modules:
  0.0 198.1 jit_solution(15107310221342891865)
XLA Ops:
  0.0 6.6 %copy.10 = f32[128,6,2048]{0,2,1:T(8,128)} copy(f32[128,6,2048]{2,0,1:T(8,128)} %param.1) | data formatting | bytes 12582912 | tf_op args[0]
  6.6 5.3 %fusion.1 = f32[128,12288]{1,0:T(8,128)S(1)} fusion(f32[128,12288]{0,1:T(8,128)} %bitcast.15), kind=kOutput, calls=%fused_computation.7 | convolution fusion | flops 2415951872 | bytes 12582912 | tf_op jit(solution)/shard_map/dot_general | solution.py:74
  11.9 0.0 copy-start
  11.9 2.7 %copy-done = f32[128,12288]{1,0:T(8,128)} copy-done((f32[128,12288]{1,0:T(8,128)}, f32[128,12288]{1,0:T(8,128)S(1)}, u32[]{:S(2)}) %copy-start) | copy-done | bytes 6291480
  14.6 0.1 slice_reduce_fusion
  14.7 0.7 broadcast_in_dim.17
  15.5 4.8 %all-to-all-start = ((f32[4,6,2048]{2,1,0:T(8,128)}), f32[4,6,2048]{2,1,0:T(8,128)S(1)}, u32[]{:S(2)}, u32[]{:S(2)}) async-start(f32[4,6,2048]{2,1,0:T(8,128)} %broadcast_in_dim.17), calls=%async_computation | async-start | bytes 524288 | tf_op jit(solution)/shard_map/all_to_all | solution.py:37
  20.3 6.6 %copy.11 = f32[128,12288]{0,1:T(8,128)} copy(f32[128,12288]{1,0:T(8,128)} %copy-done) | data formatting | bytes 12582912 | tf_op jit(solution)/shard_map/dot_general | solution.py:74
  26.9 0.0 all-to-all-done
  26.9 0.1 broadcast_select_fusion
  27.0 0.1 add.19
  27.1 4.4 %broadcast_add_fusion = f32[128,6,64,32]{0,3,2,1:T(8,128)S(1)} fusion(f32[128,6,64,32]{0,3,2,1:T(8,128)} %bitcast.13, f32[6,64,32]{2,1,0:T(8,128)S(1)} %add.19), kind=kLoop, calls=%fused_computation | loop fusion | flops 1572864 | bytes 12632064 | tf_op jit(solution)/shard_map/add | solution.py:80
  31.6 1.0 copy.12
  32.6 8.8 %all_to_all.15 = f32[32,2,128,6,32]{2,4,0,3,1:T(8,128)S(1)} all-to-all(f32[32,2,128,6,32]{2,4,0,3,1:T(8,128)S(1)} %copy.12), channel_id=1, replica_groups=mesh['space_0'=8,'space_1'=4,'space_2'=2,'tm'=4] {'space_2'}, dimensions={1} | all-to-all | bytes 12582912 | tf_op jit(solution)/shard_map/all_to_all | solution.py:25
  41.4 1.0 copy.13
  42.4 152.2 %all_to_all.16 = f32[32,2,128,6,32]{2,4,1,3,0:T(8,128)S(1)} all-to-all(f32[32,2,128,6,32]{2,4,1,3,0:T(8,128)S(1)} %copy.13), channel_id=1, replica_groups=mesh['space_0'=8,'space_1'=4,'space_2'=2,'tm'=4] {'space_0','space_1'}, dimensions={0} | all-to-all | bytes 12582912 | tf_op jit(solution)/shard_map/all_to_all | solution.py:25
  194.7 3.4 %copy.14 = f32[32,2,128,6,32]{2,4,3,1,0:T(8,128)} copy(f32[32,2,128,6,32]{2,4,1,3,0:T(8,128)S(1)} %all_to_all.16) | data formatting | bytes 12582912 | tf_op jit(solution)/shard_map/all_to_all | solution.py:25
  (4 shorter events, 0.0 us)
Async XLA Ops:
  11.9 2.7 %copy-start = (f32[128,12288]{1,0:T(8,128)}, f32[128,12288]{1,0:T(8,128)S(1)}, u32[]{:S(2)}) copy-start(f32[128,12288]{1,0:T(8,128)S(1)} %fusion.1) | copy-start | bytes 18874372
  15.5 11.4 %all-to-all-start = ((f32[4,6,2048]{2,1,0:T(8,128)}), f32[4,6,2048]{2,1,0:T(8,128)S(1)}, u32[]{:S(2)}, u32[]{:S(2)}) async-start(f32[4,6,2048]{2,1,0:T(8,128)} %broadcast_in_dim.17), calls=%async_computation | async-start | bytes 524288 | tf_op jit(solution)/shard_map/all_to_all | solution.py:37
where the time goes:
time: 198 us
  blocking collectives  161 us (81%)
  local copies, waits for them, and re-layouts  22.3 us (11%)
  matrix products  5.31 us (3%)
  starting transfers between devices  4.82 us (2%)
  other arithmetic  4.54 us (2%)
    all_to_all x2, blocking collectives, moved_by_axis(): lax.all_to_all(pieces, axes[k], split_axis=k, concat_axis=k, tiled=True)  161 us
    unnamed x3, local copies, waits for them, and re-layouts  9.25 us
    dot_general x1, local copies, waits for them, and re-layouts, per_device(): jnp.dot(upper_ones.T, flat_days, precision=lax.Precision.HIGHEST, preferr...  6.59 us
    dot_general x1, matrix products, per_device(): jnp.dot(upper_ones.T, flat_days, precision=lax.Precision.HIGHEST, preferr...  5.31 us
    all_to_all x1, starting transfers between devices, from_everyone(): return lax.all_to_all(copies, axis, split_axis=0, concat_axis=0, tiled=True)  4.82 us
    all_to_all x2, local copies, waits for them, and re-layouts, moved_by_axis(): lax.all_to_all(pieces, axes[k], split_axis=k, concat_axis=k, tiled=True)  4.46 us
    add x1, other arithmetic, per_device(): return jnp.transpose(rechunk(running + carried[None]), (1, 2, 0))  4.42 us
  transfers between devices with their start and end apart: 1, of which 0 were waited for; matrix products, arithmetic and copies ran while one was open for 3% of the time, Pallas kernels for 0%

commit v1 on v0

v1 whole, which is shorter than its diff:
```python
import functools

import jax
import jax.numpy as jnp
from jax import lax
from jax.experimental import pallas as pl
from jax.experimental.pallas import tpu as pltpu
from jax.sharding import Mesh
from jax.sharding import PartitionSpec as P

PLANE = ("space_1", "space_2")
EARLY = (3, -3)
NEAR = (1, -1)
PLANE_FIRST = (0, 4, 2, -2)

IN_VMEM = pl.BlockSpec(memory_space=pltpu.VMEM)
IN_HBM = pl.BlockSpec(memory_space=pl.ANY)
IN_SMEM = pl.BlockSpec(memory_space=pltpu.SMEM)
TOKEN = (8, 128)
LIMIT = pltpu.CompilerParams(vmem_limit_bytes=12 * 2**20)


def vmem(shape):
    return pltpu.VMEM(shape, jnp.float32)


def hbm(shape):
    return pltpu.HBM(shape, jnp.float32)


def ring_place(where_ref, step, ring):
    return lax.rem(where_ref[0] + (step + ring), ring)


def carried(theirs_ref, blocks_before, row, lanes):
    carry = None
    for q in range(theirs_ref.shape[0]):
        line = jnp.where(q < blocks_before, theirs_ref[q, pl.ds(row, 1), lanes], 0.0)
        carry = line if carry is None else carry + line
    return carry


def running_kernel(where_ref, days_ref, theirs_ref, *refs, steps, ring, stacked):
    n = len(steps)
    *out_refs, done_ref, days_buf, out_buf, in_sems, out_sems = refs
    rows, days, lon = days_ref.shape
    width = lon // ring
    plane, cell = out_buf.shape[1], out_buf.shape[3]
    lanes = [
        pl.ds(pl.multiple_of(ring_place(where_ref, s, ring) * width, width), width) for s in steps
    ]
    reads = [
        [
            pltpu.make_async_copy(days_ref.at[r, :, lanes[k]], days_buf.at[k, r], in_sems.at[k, r])
            for r in range(rows)
        ]
        for k in range(n)
    ]
    writes = [
        pltpu.make_async_copy(
            out_buf.at[k], out_refs[0].at[:, k] if stacked else out_refs[k], out_sems.at[k]
        )
        for k in range(n)
    ]
    for line in reads:
        for copy in line:
            copy.start()
    earlier = lax.broadcasted_iota(jnp.int32, (days, days), 0)
    later = lax.broadcasted_iota(jnp.int32, (days, days), 1)
    upto = (earlier <= later).astype(jnp.bfloat16)
    first = lax.broadcasted_iota(jnp.int32, (days, width), 0) == 0
    dot = functools.partial(jnp.dot, preferred_element_type=jnp.float32)
    for k in range(n):
        for r in range(rows):
            reads[k][r].wait()
            x = days_buf[k, r]
            if theirs_ref is not None:
                x = jnp.where(first, x + carried(theirs_ref, where_ref[1], r, lanes[k]), x)
            x = x.T
            high = x.astype(jnp.bfloat16)
            rest = x - high.astype(jnp.float32)
            mid = rest.astype(jnp.bfloat16)
            low = (rest - mid.astype(jnp.float32)).astype(jnp.bfloat16)
            total = dot(high, upto) + (dot(mid, upto) + dot(low, upto))
            out_buf[k, :, r] = total.reshape(plane, cell, days)
        writes[k].start()
    done_ref[...] = jnp.zeros_like(done_ref)
    for copy in writes:
        copy.wait()


def running(where, by_row, theirs, token, ring, steps, stacked, plane):
    rows, days, lon = by_row.shape
    width = lon // ring
    cell = width // plane
    n = len(steps)
    outs = [hbm((plane, n, rows, cell, days))] if stacked else [hbm((plane, rows, cell, days))] * n
    args = [where, by_row]
    specs = [IN_SMEM, IN_HBM]
    for extra in (theirs, token):
        if extra is not None:
            args.append(extra)
            specs.append(IN_VMEM)

    def body(where_ref, days_ref, *refs):
        refs = list(refs)
        theirs_ref = None if theirs is None else refs.pop(0)
        if token is not None:
            refs.pop(0)
        running_kernel(where_ref, days_ref, theirs_ref, *refs, steps=steps, ring=ring, stacked=stacked)

    *made, done = pl.pallas_call(
        body,
        compiler_params=LIMIT,
        in_specs=specs,
        out_specs=[IN_HBM] * len(outs) + [IN_VMEM],
        out_shape=[*outs, jax.ShapeDtypeStruct(TOKEN, jnp.float32)],
        scratch_shapes=[
            pltpu.VMEM((n, rows, days, width), jnp.float32),
            pltpu.VMEM((n, plane, rows, cell, days), jnp.float32),
            pltpu.SemaphoreType.DMA((n, rows)),
            pltpu.SemaphoreType.DMA((n,)),
        ],
    )(*args)
    return made, done


def totals_kernel(days_ref, token_ref, total_ref, days_buf, sems):
    rows, _, lon = days_ref.shape
    cuts = sems.shape[0]
    width = lon // cuts
    copies = [
        pltpu.make_async_copy(
            days_ref.at[:, :, pl.ds(c * width, width)], days_buf.at[:, :, pl.ds(c * width, width)], sems.at[c]
        )
        for c in range(cuts)
    ]
    for copy in copies:
        copy.start()
    for c in range(cuts):
        copies[c].wait()
        for r in range(rows):
            line = jnp.sum(days_buf[r, :, pl.ds(c * width, width)], axis=0, keepdims=True)
            for q in range(total_ref.shape[0]):
                total_ref[q, pl.ds(r, 1), pl.ds(c * width, width)] = line


def block_totals(by_row, token, copies, cuts=8):
    rows, _, lon = by_row.shape
    return pl.pallas_call(
        totals_kernel,
        compiler_params=LIMIT,
        in_specs=[IN_HBM, IN_VMEM],
        out_specs=IN_VMEM,
        out_shape=vmem((copies, rows, lon)),
        scratch_shapes=[pltpu.VMEM(by_row.shape, jnp.float32), pltpu.SemaphoreType.DMA((cuts,))],
    )(by_row, (token))


def lines_kernel(where_ref, theirs_ref, token_ref, *refs, steps, ring):
    *line_refs, done_ref = refs
    width = theirs_ref.shape[2] // ring
    for step, line_ref in zip(steps, line_refs):
        lanes = pl.ds(pl.multiple_of(ring_place(where_ref, step, ring) * width, width), width)
        line_ref[...] = jnp.zeros_like(line_ref)
        for r in range(theirs_ref.shape[1]):
            line_ref[pl.ds(r, 1)] = carried(theirs_ref, where_ref[1], r, lanes)
    done_ref[...] = jnp.zeros_like(done_ref)


def carry_lines(where, theirs, token, steps, ring):
    width = theirs.shape[2] // ring
    *lines, done = pl.pallas_call(
        functools.partial(lines_kernel, steps=steps, ring=ring),
        compiler_params=LIMIT,
        in_specs=[IN_SMEM, IN_VMEM, IN_VMEM],
        out_specs=[IN_VMEM] * (len(steps) + 1),
        out_shape=[vmem((8, width))] * len(steps) + [vmem(TOKEN)],
    )(where, (theirs), (token))
    return lines, done


def gather_kernel(*refs):
    *refs, out_ref = refs
    plane, n, _, cell, days = out_ref.shape
    block_refs, line_refs = refs[:n], refs[n:-1]
    row = pl.program_id(0)
    for k in range(n):
        block = block_refs[k][:, 0]
        if k < len(line_refs):
            carry = jnp.broadcast_to(line_refs[k][pl.ds(row, 1)], (days, plane * cell)).T
            block = block + carry.reshape(plane, cell, days)
        out_ref[:, k, 0] = block


def gathered(blocks, lines, token):
    plane, rows, cell, days = blocks[0].shape
    n = len(blocks)
    return pl.pallas_call(
        gather_kernel,
        compiler_params=LIMIT,
        grid=(rows,),
        in_specs=[pl.BlockSpec((plane, 1, cell, days), lambda r: (0, r, 0, 0))] * n
        + [pl.BlockSpec(line.shape, lambda r: (0, 0)) for line in lines]
        + [pl.BlockSpec(memory_space=pl.ANY)],
        out_specs=pl.BlockSpec((plane, n, 1, cell, days), lambda r: (0, 0, r, 0, 0)),
        out_shape=jax.ShapeDtypeStruct((plane, n, rows, cell, days), jnp.float32),
    )(*blocks, *lines, token)


def place_kernel(where_ref, piece_ref, *refs):
    refs[-1][...] = piece_ref[...].reshape(refs[-1].shape)


def place(where, whole, ring, piece, steps):
    plane, _, rows, cell, days = piece.shape
    half = plane // 2

    def target(j, h, where):
        step = jnp.int32(steps[0])
        for i, s in enumerate(steps[1:], 1):
            step = jnp.where(j == i, s, step)
        return (lax.rem(where[0] - step + 2 * ring, ring), h, 0, 0, 0)

    args = (where, piece) if whole is None else (where, piece, whole)
    in_specs = [pl.BlockSpec((half, 1, rows, cell, days), lambda j, h, where: (h, j, 0, 0, 0))]
    if whole is not None:
        in_specs.append(pl.BlockSpec(memory_space=pl.ANY))
    return pl.pallas_call(
        place_kernel,
        compiler_params=LIMIT,
        grid_spec=pltpu.PrefetchScalarGridSpec(
            num_scalar_prefetch=1,
            grid=(len(steps), 2),
            in_specs=in_specs,
            out_specs=pl.BlockSpec((1, half, rows, cell, days), target),
        ),
        out_shape=jax.ShapeDtypeStruct((ring, plane, rows, cell, days), jnp.float32),
        input_output_aliases={} if whole is None else {2: 0},
    )(*args)


def place_block(where, whole, block, step):
    ring = whole.shape[0]
    at = lax.rem(where[0] - step + ring, ring)
    return lax.dynamic_update_slice(whole, block[None], (at, 0, 0, 0, 0))


def shifted(block, ring, step):
    return lax.ppermute(block, "space_0", [(i, (i + step) % ring) for i in range(ring)])


def exchanged(value, axes):
    return lax.all_to_all(value, axes, split_axis=0, concat_axis=0, tiled=True)


def per_device(precip):
    by_row = jnp.transpose(precip, (1, 0, 2))
    by_row = pltpu.with_memory_space_constraint(by_row, pltpu.HBM)
    rows, days, lon = by_row.shape
    ring = lax.axis_size("space_0")
    plane = lax.axis_size("space_1") * lax.axis_size("space_2")
    blocks = lax.axis_size("tm")
    where = jnp.stack([lax.axis_index("space_0"), lax.axis_index("tm")]).astype(jnp.int32)

    def sent(block, step):
        return shifted(block, ring, step)

    early, token = running(where, by_row, None, None, ring, EARLY, False, plane)
    early = [sent(block, step) for block, step in zip(early, EARLY)]
    theirs = block_totals(by_row, token, blocks)
    theirs = exchanged(theirs, "tm")
    (first,), token = running(where, by_row, theirs, None, ring, PLANE_FIRST, True, plane)
    mixed = exchanged(first, PLANE)
    near, token = running(where, by_row, theirs, token, ring, NEAR, False, plane)
    near = [sent(block, step) for block, step in zip(near, NEAR)]
    lines, token = carry_lines(where, theirs, token, EARLY, ring)
    lines = [sent(line, step) for line, step in zip(lines, EARLY)]
    late = [sent(mixed[:, k], PLANE_FIRST[k]) for k in (1, 2, 3)]
    second = gathered([*early, *near], lines, token)
    second = exchanged(second, PLANE)
    whole = place(where, None, ring, mixed, (0,))
    whole = place(where, whole, ring, second, (*EARLY, *NEAR))
    for k in (3, 2, 1):
        whole = place_block(where, whole, late[k - 1], PLANE_FIRST[k])
    return whole.reshape(ring * plane * rows, lon // (ring * plane), days)


def solution(mesh):
    finer = Mesh(
        mesh.devices.reshape(8, 4, 2, mesh.shape["tm"]), ("space_0", "space_1", "space_2", "tm")
    )
    space = ("space_0", "space_1", "space_2")
    return jax.shard_map(
        per_device,
        mesh=finer,
        in_specs=(P("tm", space, None),),
        out_specs=P(None, space, "tm"),
        check_vma=False,
    )
```

time: 198 us -> 206 us (1.040); the launches traced: 198 us -> 204 us
  blocking collectives: 161 us -> 9.85 us
  waiting for transfers between devices: 0.01 us -> 114 us
  Pallas kernels: 0 us -> 35.9 us
  starting transfers between devices: 4.82 us -> 34.4 us
  local copies, waits for them, and re-layouts: 22.3 us -> 9.36 us
  matrix products: 5.31 us -> 0 us
  other arithmetic: 4.54 us -> 0.07 us
    all_to_all x2 -> x1, blocking collectives: 161 us -> 9.85 us  [exchanged(): return lax.all_to_all(value, axes, split_axis=0, concat_axis=0, tiled=True)]
    ppermute x0 -> x9, waiting for transfers between devices: none -> 87.8 us  [shifted(): lax.ppermute(block, 'space_0', [(i, (i + step) % ring) for i in range(rin...]
    pallas_call x0 -> x8, Pallas kernels: none -> 35.9 us  [the longest x3 22.8 us: running(): pl.pallas_call(body, compiler_params=LIMIT, in_specs=specs, out_specs=[IN...]
    all_to_all x1 -> x2, waiting for transfers between devices: 0.01 us -> 26.2 us  [exchanged(): return lax.all_to_all(value, axes, split_axis=0, concat_axis=0, tiled=True)]
    ppermute x0 -> x9, starting transfers between devices: none -> 24.6 us  [shifted(): lax.ppermute(block, 'space_0', [(i, (i + step) % ring) for i in range(rin...]
    unnamed x3 -> x2, local copies, waits for them, and re-layouts: 9.25 us -> 1.67 us
    dot_general x1 -> x0, local copies, waits for them, and re-layouts: 6.59 us -> none  [per_device(): jnp.dot(upper_ones.T, flat_days, precision=lax.Precision.HIGHEST, preferr...]
    dynamic_update_slice x0 -> x3, local copies, waits for them, and re-layouts: none -> 6.19 us  [place_block(): return lax.dynamic_update_slice(whole, block[None], (at, 0, 0, 0, 0))]
  transfers between devices with their start and end apart: 1 -> 11, of which waited for: 0 -> 4; matrix products, arithmetic and copies ran while one was open for 3% -> 3% of each run, Pallas kernels for 0% -> 8%
where the time goes in v1:
time: 206 us; the launch traced here: 204 us
  waiting for transfers between devices  114 us (55%)
  Pallas kernels  35.9 us (17%)
  starting transfers between devices  34.4 us (17%)
  blocking collectives  9.85 us (5%)
  local copies, waits for them, and re-layouts  9.36 us (5%)
    ppermute x9, waiting for transfers between devices, shifted(): lax.ppermute(block, 'space_0', [(i, (i + step) % ring) for i in range(rin...  87.8 us
    all_to_all x2, waiting for transfers between devices, exchanged(): return lax.all_to_all(value, axes, split_axis=0, concat_axis=0, tiled=True)  26.2 us
    ppermute x9, starting transfers between devices, shifted(): lax.ppermute(block, 'space_0', [(i, (i + step) % ring) for i in range(rin...  24.6 us
    pallas_call x3, Pallas kernels, running(): pl.pallas_call(body, compiler_params=LIMIT, in_specs=specs, out_specs=[IN...  22.8 us
    all_to_all x1, blocking collectives, exchanged(): return lax.all_to_all(value, axes, split_axis=0, concat_axis=0, tiled=True)  9.85 us
    all_to_all x2, starting transfers between devices, exchanged(): return lax.all_to_all(value, axes, split_axis=0, concat_axis=0, tiled=True)  9.73 us
    pallas_call x2, Pallas kernels, place(): pl.pallas_call(place_kernel, compiler_params=LIMIT, grid_spec=pltpu.Prefe...  8.22 us
    dynamic_update_slice x3, local copies, waits for them, and re-layouts, place_block(): return lax.dynamic_update_slice(whole, block[None], (at, 0, 0, 0, 0))  6.19 us
  transfers between devices with their start and end apart: 11, of which 4 were waited for; matrix products, arithmetic and copies ran while one was open for 3% of the time, Pallas kernels for 8%

profile of v1, /device:TPU:10, one launch (start us, length us, event | category | flops | bytes accessed | tf_op | source)
XLA Modules:
  0.0 203.6 jit_solution(5622923944392089454)
XLA Ops:
  0.0 0.1 pad_add_fusion.where_ref
  0.1 6.2 %shard_map.17 = (f32[8,6,32,128]{3,2,1,0:T(8,128)}, f32[8,6,32,128]{3,2,1,0:T(8,128)}, f32[8,128]{1,0:T(8,128)S(1)}) custom-call(s32[2]{0:T(128)S(1)} %pad_add_fusion.where_ref, f32[6,128,2048]{2,1,0:T(8,128)} %bitcast.22), custom_call_target="tpu_custom_call" | custom-call | tf_op jit(solution)/shard_map/pallas_call | solution.py:112
  6.3 3.0 %shard_map.18 = f32[4,6,2048]{2,1,0:T(8,128)S(1)} custom-call(f32[6,128,2048]{2,1,0:T(8,128)} %bitcast.23, f32[8,128]{1,0:T(8,128)S(1)} %get-tuple-element.18.token_ref), custom_call_target="tpu_custom_call" | custom-call | tf_op jit(solution)/shard_map/pallas_call | solution.py:150
  9.2 9.8 %all_to_all.15.refs_0_.theirs_ref = f32[4,6,2048]{2,1,0:T(8,128)S(1)} all-to-all(f32[4,6,2048]{2,1,0:T(8,128)S(1)} %shard_map.18), channel_id=1, replica_groups=mesh['space_0'=8,'space_1'=4,'space_2'=2,'tm'=4] {'tm'}, dimensions={0} | all-to-all | bytes 393216 | tf_op jit(solution)/shard_map/all_to_all | solution.py:254
  19.1 10.3 %shard_map.19 = (f32[8,4,6,32,128]{4,3,2,1,0:T(8,128)}, f32[8,128]{1,0:T(8,128)S(1)}) custom-call(s32[2]{0:T(128)S(1)} %pad_add_fusion.where_ref, f32[6,128,2048]{2,1,0:T(8,128)} %bitcast.24, f32[4,6,2048]{2,1,0:T(8,128)S(1)} %all_to_all.15.refs_0_.theirs_ref), custom_call_target="tpu_custom_call" | custom-call | tf_op jit(solution)/shard_map/pallas_call | solution.py:112
  29.4 4.9 %all-to-all-start.2 = ((f32[8,4,6,32,128]{4,3,2,1,0:T(8,128)}), f32[8,4,6,32,128]{4,3,2,1,0:T(8,128)S(1)}, u32[]{:S(2)}, u32[]{:S(2)}) async-start(f32[8,4,6,32,128]{4,3,2,1,0:T(8,128)} %get-tuple-element.26), calls=%async_computation.2 | async-start | bytes 6291456 | tf_op jit(solution)/shard_map/all_to_all | solution.py:254
  34.3 4.6 %collective-permute-start = (f32[8,6,32,128]{3,2,1,0:T(8,128)}, f32[8,6,32,128]{3,2,1,0:T(8,128)S(1)}, u32[]{:S(2)}, u32[]{:S(2)}) collective-permute-start(f32[8,6,32,128]{3,2,1,0:T(8,128)} %get-tuple-element.16), channel_id=1, source_target_pairs={{0,96},{32,128},{64,160},{96,192},{128,224},{160,0},{192,32},{224,... | collective-permute-start | bytes 2359304 | tf_op jit(solution)/shard_map/ppermute | solution.py:250
  38.9 2.1 %collective-permute-start.1 = (f32[8,6,32,128]{3,2,1,0:T(8,128)}, f32[8,6,32,128]{3,2,1,0:T(8,128)S(1)}, u32[]{:S(2)}, u32[]{:S(2)}) collective-permute-start(f32[8,6,32,128]{3,2,1,0:T(8,128)} %get-tuple-element.17), channel_id=1, source_target_pairs={{0,160},{32,192},{64,224},{96,0},{128,32},{160,64},{192,96},{224,1... | collective-permute-start | bytes 2359304 | tf_op jit(solution)/shard_map/ppermute | solution.py:250
  41.1 6.3 %shard_map.20 = (f32[8,6,32,128]{3,2,1,0:T(8,128)}, f32[8,6,32,128]{3,2,1,0:T(8,128)}, f32[8,128]{1,0:T(8,128)S(1)}) custom-call(s32[2]{0:T(128)S(1)} %pad_add_fusion.where_ref, f32[6,128,2048]{2,1,0:T(8,128)} %bitcast.25, f32[4,6,2048]{2,1,0:T(8,128)S(1)} %all_to_all.15.refs_0_.theirs_ref, f32[8,128]{1,0:T(8,128)S(1)} %get-tuple-element.19.refs_1_), custom_call_target="tpu_custom_call" | custom-call | tf_op jit(solution)/shard_map/pallas_call | solution.py:112
  47.4 1.1 collective-permute-start.2
  48.5 2.2 %collective-permute-start.3 = (f32[8,6,32,128]{3,2,1,0:T(8,128)}, f32[8,6,32,128]{3,2,1,0:T(8,128)S(1)}, u32[]{:S(2)}, u32[]{:S(2)}) collective-permute-start(f32[8,6,32,128]{3,2,1,0:T(8,128)} %get-tuple-element.21), channel_id=1, source_target_pairs={{0,224},{32,0},{64,32},{96,64},{128,96},{160,128},{192,160},{224,1... | collective-permute-start | bytes 2359304 | tf_op jit(solution)/shard_map/ppermute | solution.py:250
  50.7 0.6 shard_map.21
  51.3 2.9 %collective-permute-start.4 = (f32[8,256]{1,0:T(8,128)S(1)}, f32[8,256]{1,0:T(8,128)S(1)}, u32[]{:S(2)}, u32[]{:S(2)}) collective-permute-start(f32[8,256]{1,0:T(8,128)S(1)} %get-tuple-element.23), channel_id=1, source_target_pairs={{0,96},{32,128},{64,160},{96,192},{128,224},{160,0},{192,32},{224,... | collective-permute-start | bytes 24584 | tf_op jit(solution)/shard_map/ppermute | solution.py:250
  54.2 56.1 %collective-permute-done.4.refs_4_ = f32[8,256]{1,0:T(8,128)S(1)} collective-permute-done((f32[8,256]{1,0:T(8,128)S(1)}, f32[8,256]{1,0:T(8,128)S(1)}, u32[]{:S(2)}, u32[]{:S(2)}) %collective-permute-start.4) | collective-permute-done | bytes 8224 | tf_op jit(solution)/shard_map/ppermute | solution.py:250
  110.2 3.9 %collective-permute-start.5 = (f32[8,256]{1,0:T(8,128)S(1)}, f32[8,256]{1,0:T(8,128)S(1)}, u32[]{:S(2)}, u32[]{:S(2)}) collective-permute-start(f32[8,256]{1,0:T(8,128)S(1)} %get-tuple-element.24), channel_id=1, source_target_pairs={{0,160},{32,192},{64,224},{96,0},{128,32},{160,64},{192,96},{224,1... | collective-permute-start | bytes 24584 | tf_op jit(solution)/shard_map/ppermute | solution.py:250
  114.1 1.6 collective-permute-done.5.refs_5_
  115.7 0.0 collective-permute-done.refs_0_
  115.7 0.0 collective-permute-done.1.refs_1_
  115.7 0.0 collective-permute-done.2.refs_2_
  115.7 1.3 shard_map.22
  117.1 1.7 copy-done
  118.7 4.8 %all-to-all-start.1 = ((f32[8,4,6,32,128]{4,3,2,1,0:T(8,128)}), f32[8,4,6,32,128]{4,3,2,1,0:T(8,128)}, u32[]{:S(2)}, u32[]{:S(2)}) async-start(f32[8,4,6,32,128]{4,3,2,1,0:T(8,128)} %copy-done), calls=%async_computation.1 | async-start | bytes 6291456 | tf_op jit(solution)/shard_map/all_to_all | solution.py:254
  123.5 1.5 slice_bitcast_fusion
  125.0 5.5 %collective-permute-start.6 = (f32[8,6,32,128]{3,2,1,0:T(8,128)}, f32[8,6,32,128]{3,2,1,0:T(8,128)}, u32[]{:S(2)}, u32[]{:S(2)}) collective-permute-start(f32[8,6,32,128]{3,2,1,0:T(8,128)} %get-tuple-element.29), channel_id=1, source_target_pairs={{0,192},{32,224},{64,0},{96,32},{128,64},{160,96},{192,128},{224,1... | collective-permute-start | bytes 2359304 | tf_op jit(solution)/shard_map/ppermute | solution.py:250
  130.5 2.4 %collective-permute-start.8 = (f32[8,6,32,128]{3,2,1,0:T(8,128)}, f32[8,6,32,128]{3,2,1,0:T(8,128)}, u32[]{:S(2)}, u32[]{:S(2)}) collective-permute-start(f32[8,6,32,128]{3,2,1,0:T(8,128)} %get-tuple-element.27), channel_id=1, source_target_pairs={{0,128},{32,160},{64,192},{96,224},{128,0},{160,32},{192,64},{224,... | collective-permute-start | bytes 2359304 | tf_op jit(solution)/shard_map/ppermute | solution.py:250
  132.9 1.5 shard_map.23.refs_0_
  134.4 26.2 %all-to-all-done.1.piece_ref = f32[8,4,6,32,128]{4,3,2,1,0:T(8,128)} async-done(((f32[8,4,6,32,128]{4,3,2,1,0:T(8,128)}), f32[8,4,6,32,128]{4,3,2,1,0:T(8,128)}, u32[]{:S(2)}, u32[]{:S(2)}) %all-to-all-start.1) | async-done | bytes 3145760 | tf_op jit(solution)/shard_map/all_to_all | solution.py:254
  160.6 6.7 %shard_map.24 = f32[8,8,6,32,128]{4,3,2,1,0:T(8,128)} custom-call(s32[2]{0:T(128)S(1)} %pad_add_fusion.where_ref, f32[8,4,6,32,128]{4,3,2,1,0:T(8,128)} %all-to-all-done.1.piece_ref, f32[8,8,6,32,128]{4,3,2,1,0:T(8,128)} %shard_map.23.refs_0_), custom_call_target="tpu_custom_call", output_to_operand_aliasing={{}: (2, {})} | custom-call | tf_op jit(solution)/shard_map/pallas_call | solution.py:229
  167.3 30.1 %collective-permute-done.6 = f32[8,6,32,128]{3,2,1,0:T(8,128)} collective-permute-done((f32[8,6,32,128]{3,2,1,0:T(8,128)}, f32[8,6,32,128]{3,2,1,0:T(8,128)}, u32[]{:S(2)}, u32[]{:S(2)}) %collective-permute-start.6) | collective-permute-done | bytes 786464 | tf_op jit(solution)/shard_map/ppermute | solution.py:250
  197.4 2.1 %bitcast_dynamic-update-slice_fusion.2 = f32[8,8,6,32,128]{4,3,2,1,0:T(8,128)} fusion(f32[8,8,6,32,128]{4,3,2,1,0:T(8,128)} %shard_map.24, s32[]{:T(128)S(6)} %select_n.9, f32[8,6,32,128]{3,2,1,0:T(8,128)} %collective-permute-done.6), kind=kLoop, calls=%fused_computation.5 | loop fusion | bytes 1572868 | tf_op jit(solution)/shard_map/dynamic_update_slice | solution.py:246
  199.5 2.1 %bitcast_dynamic-update-slice_fusion.1 = f32[8,8,6,32,128]{4,3,2,1,0:T(8,128)} fusion(f32[8,8,6,32,128]{4,3,2,1,0:T(8,128)} %bitcast_dynamic-update-slice_fusion.2, s32[]{:T(128)S(6)} %select_n.10, f32[8,6,32,128]{3,2,1,0:T(8,128)} %collective-permute-done.7), kind=kLoop, calls=%fused_computation.4 | loop fusion | bytes 1572868 | tf_op jit(solution)/shard_map/dynamic_update_slice | solution.py:246
  201.5 2.1 %bitcast_dynamic-update-slice_fusion = f32[8,8,6,32,128]{4,3,2,1,0:T(8,128)} fusion(f32[8,8,6,32,128]{4,3,2,1,0:T(8,128)} %bitcast_dynamic-update-slice_fusion.1, s32[]{:T(128)S(6)} %select_n.11, f32[8,6,32,128]{3,2,1,0:T(8,128)} %collective-permute-done.8), kind=kLoop, calls=%fused_computation.3 | loop fusion | bytes 1572868 | tf_op jit(solution)/shard_map/dynamic_update_slice | solution.py:246
  (6 shorter events, 0.0 us)
Async XLA Ops:
  29.4 89.4 %all-to-all-start.2 = ((f32[8,4,6,32,128]{4,3,2,1,0:T(8,128)}), f32[8,4,6,32,128]{4,3,2,1,0:T(8,128)S(1)}, u32[]{:S(2)}, u32[]{:S(2)}) async-start(f32[8,4,6,32,128]{4,3,2,1,0:T(8,128)} %get-tuple-element.26), calls=%async_computation.2 | async-start | bytes 6291456 | tf_op jit(solution)/shard_map/all_to_all | solution.py:254
  34.3 81.4 %collective-permute-start = (f32[8,6,32,128]{3,2,1,0:T(8,128)}, f32[8,6,32,128]{3,2,1,0:T(8,128)S(1)}, u32[]{:S(2)}, u32[]{:S(2)}) collective-permute-start(f32[8,6,32,128]{3,2,1,0:T(8,128)} %get-tuple-element.16), channel_id=1, source_target_pairs={{0,96},{32,128},{64,160},{96,192},{128,224},{160,0},{192,32},{224,... | collective-permute-start | bytes 2359304 | tf_op jit(solution)/shard_map/ppermute | solution.py:250
  38.9 76.8 %collective-permute-start.1 = (f32[8,6,32,128]{3,2,1,0:T(8,128)}, f32[8,6,32,128]{3,2,1,0:T(8,128)S(1)}, u32[]{:S(2)}, u32[]{:S(2)}) collective-permute-start(f32[8,6,32,128]{3,2,1,0:T(8,128)} %get-tuple-element.17), channel_id=1, source_target_pairs={{0,160},{32,192},{64,224},{96,0},{128,32},{160,64},{192,96},{224,1... | collective-permute-start | bytes 2359304 | tf_op jit(solution)/shard_map/ppermute | solution.py:250
  47.4 68.3 %collective-permute-start.2 = (f32[8,6,32,128]{3,2,1,0:T(8,128)}, f32[8,6,32,128]{3,2,1,0:T(8,128)S(1)}, u32[]{:S(2)}, u32[]{:S(2)}) collective-permute-start(f32[8,6,32,128]{3,2,1,0:T(8,128)} %get-tuple-element.20), channel_id=1, source_target_pairs={{0,32},{32,64},{64,96},{96,128},{128,160},{160,192},{192,224},{224... | collective-permute-start | bytes 2359304 | tf_op jit(solution)/shard_map/ppermute | solution.py:250
  48.5 67.2 %collective-permute-start.3 = (f32[8,6,32,128]{3,2,1,0:T(8,128)}, f32[8,6,32,128]{3,2,1,0:T(8,128)S(1)}, u32[]{:S(2)}, u32[]{:S(2)}) collective-permute-start(f32[8,6,32,128]{3,2,1,0:T(8,128)} %get-tuple-element.21), channel_id=1, source_target_pairs={{0,224},{32,0},{64,32},{96,64},{128,96},{160,128},{192,160},{224,1... | collective-permute-start | bytes 2359304 | tf_op jit(solution)/shard_map/ppermute | solution.py:250
  51.3 59.0 %collective-permute-start.4 = (f32[8,256]{1,0:T(8,128)S(1)}, f32[8,256]{1,0:T(8,128)S(1)}, u32[]{:S(2)}, u32[]{:S(2)}) collective-permute-start(f32[8,256]{1,0:T(8,128)S(1)} %get-tuple-element.23), channel_id=1, source_target_pairs={{0,96},{32,128},{64,160},{96,192},{128,224},{160,0},{192,32},{224,... | collective-permute-start | bytes 24584 | tf_op jit(solution)/shard_map/ppermute | solution.py:250
  110.2 5.5 %collective-permute-start.5 = (f32[8,256]{1,0:T(8,128)S(1)}, f32[8,256]{1,0:T(8,128)S(1)}, u32[]{:S(2)}, u32[]{:S(2)}) collective-permute-start(f32[8,256]{1,0:T(8,128)S(1)} %get-tuple-element.24), channel_id=1, source_target_pairs={{0,160},{32,192},{64,224},{96,0},{128,32},{160,64},{192,96},{224,1... | collective-permute-start | bytes 24584 | tf_op jit(solution)/shard_map/ppermute | solution.py:250
  117.1 1.7 copy-start
  118.7 41.9 %all-to-all-start.1 = ((f32[8,4,6,32,128]{4,3,2,1,0:T(8,128)}), f32[8,4,6,32,128]{4,3,2,1,0:T(8,128)}, u32[]{:S(2)}, u32[]{:S(2)}) async-start(f32[8,4,6,32,128]{4,3,2,1,0:T(8,128)} %copy-done), calls=%async_computation.1 | async-start | bytes 6291456 | tf_op jit(solution)/shard_map/all_to_all | solution.py:254
  125.0 72.4 %collective-permute-start.6 = (f32[8,6,32,128]{3,2,1,0:T(8,128)}, f32[8,6,32,128]{3,2,1,0:T(8,128)}, u32[]{:S(2)}, u32[]{:S(2)}) collective-permute-start(f32[8,6,32,128]{3,2,1,0:T(8,128)} %get-tuple-element.29), channel_id=1, source_target_pairs={{0,192},{32,224},{64,0},{96,32},{128,64},{160,96},{192,128},{224,1... | collective-permute-start | bytes 2359304 | tf_op jit(solution)/shard_map/ppermute | solution.py:250
  130.5 69.0 %collective-permute-start.7 = (f32[8,6,32,128]{3,2,1,0:T(8,128)}, f32[8,6,32,128]{3,2,1,0:T(8,128)}, u32[]{:S(2)}, u32[]{:S(2)}) collective-permute-start(f32[8,6,32,128]{3,2,1,0:T(8,128)} %get-tuple-element.28), channel_id=1, source_target_pairs={{0,64},{32,96},{64,128},{96,160},{128,192},{160,224},{192,0},{224,... | collective-permute-start | bytes 2359304 | tf_op jit(solution)/shard_map/ppermute | solution.py:250
  130.5 71.0 %collective-permute-start.8 = (f32[8,6,32,128]{3,2,1,0:T(8,128)}, f32[8,6,32,128]{3,2,1,0:T(8,128)}, u32[]{:S(2)}, u32[]{:S(2)}) collective-permute-start(f32[8,6,32,128]{3,2,1,0:T(8,128)} %get-tuple-element.27), channel_id=1, source_target_pairs={{0,128},{32,160},{64,192},{96,224},{128,0},{160,32},{192,64},{224,... | collective-permute-start | bytes 2359304 | tf_op jit(solution)/shard_map/ppermute | solution.py:250

commit v2 on v1

v2 whole, which is shorter than its diff:
```python
import functools

import jax
import jax.numpy as jnp
from jax import lax
from jax.experimental import pallas as pl
from jax.experimental.pallas import tpu as pltpu
from jax.sharding import Mesh
from jax.sharding import PartitionSpec as P

PLANE = ("space_1", "space_2")
RING_FIRST = (4, 3, -3)
PLANE_FIRST = (0, 2, -2, 1, -1)
PARTS = 3

IN_VMEM = pl.BlockSpec(memory_space=pltpu.VMEM)
IN_HBM = pl.BlockSpec(memory_space=pl.ANY)
IN_SMEM = pl.BlockSpec(memory_space=pltpu.SMEM)
LIMIT = pltpu.CompilerParams(vmem_limit_bytes=12 * 2**20)


def hbm(shape):
    return pltpu.HBM(shape, jnp.float32)


def ring_place(where_ref, step, ring):
    return lax.rem(where_ref[0] + (step + ring), ring)


def carried(theirs_ref, blocks_before, row, lanes):
    carry = None
    for q in range(theirs_ref.shape[0]):
        line = jnp.where(q < blocks_before, theirs_ref[q, pl.ds(row, 1), lanes], 0.0)
        carry = line if carry is None else carry + line
    return carry


def running_kernel(sources, carry_of, out_ref, days_buf, parts_buf, out_buf, in_sems, out_sems):
    n = len(sources)
    rows, days, width = days_buf.shape[1:]
    plane, cell = out_buf.shape[1], out_buf.shape[3]
    reads = [pltpu.make_async_copy(sources[k], days_buf.at[k], in_sems.at[k]) for k in range(n)]
    writes = [
        pltpu.make_async_copy(out_buf.at[k], out_ref.at[:, k], out_sems.at[k]) for k in range(n)
    ]
    for copy in reads:
        copy.start()
    earlier = lax.broadcasted_iota(jnp.int32, (days, days), 0)
    later = lax.broadcasted_iota(jnp.int32, (days, days), 1)
    upto = (earlier <= later).astype(jnp.bfloat16)
    upto = jnp.concatenate([upto] * PARTS, 0)
    first = lax.broadcasted_iota(jnp.int32, (days, width), 0) == 0
    for k in range(n):
        reads[k].wait()
        for r in range(rows):
            x = days_buf[k, r]
            x = jnp.where(first, x + carry_of(k, r), x).T
            for p in range(PARTS):
                part = x.astype(jnp.bfloat16)
                parts_buf[k % 2, r, :, pl.ds(p * days, days)] = part
                x = x - part.astype(jnp.float32)
        for r in range(rows):
            total = jnp.dot(parts_buf[k % 2, r], upto, preferred_element_type=jnp.float32)
            out_buf[k, :, r] = total.reshape(plane, cell, days)
        writes[k].start()
    for copy in writes:
        copy.wait()


def column_kernel(where_ref, days_ref, theirs_ref, out_ref, *scratch, steps, ring):
    width = days_ref.shape[2] // ring
    lanes = [
        pl.ds(pl.multiple_of(ring_place(where_ref, s, ring) * width, width), width) for s in steps
    ]
    running_kernel(
        [days_ref.at[:, :, part] for part in lanes],
        lambda k, r: carried(theirs_ref, where_ref[1], r, lanes[k]),
        out_ref,
        *scratch,
    )


def cut_kernel(where_ref, days_ref, *refs, steps, ring):
    n = len(steps)
    out_refs, buf, in_sems, out_sems = refs[:n], refs[n], refs[n + 1], refs[n + 2]
    width = days_ref.shape[2] // ring
    reads, writes = [], []
    for k, step in enumerate(steps):
        lanes = pl.ds(pl.multiple_of(ring_place(where_ref, step, ring) * width, width), width)
        reads.append(pltpu.make_async_copy(days_ref.at[:, :, lanes], buf.at[k], in_sems.at[k]))
        writes.append(pltpu.make_async_copy(buf.at[k], out_refs[k], out_sems.at[k]))
    for copy in reads:
        copy.start()
    for read, write in zip(reads, writes):
        read.wait()
        write.start()
    for copy in writes:
        copy.wait()


def cut_columns(where, by_row, ring, steps):
    rows, days, lon = by_row.shape
    n = len(steps)
    shape = (rows, days, lon // ring)
    return pl.pallas_call(
        functools.partial(cut_kernel, steps=steps, ring=ring),
        compiler_params=LIMIT,
        in_specs=[IN_SMEM, IN_HBM],
        out_specs=[IN_HBM] * n,
        out_shape=[hbm(shape)] * n,
        scratch_shapes=[
            pltpu.VMEM((n, *shape), jnp.float32),
            pltpu.SemaphoreType.DMA((n,)),
            pltpu.SemaphoreType.DMA((n,)),
        ],
    )(where, by_row)


def block_kernel(*refs, n):
    blocks, lines, rest = refs[:n], refs[n : 2 * n], refs[2 * n :]
    out_ref, *scratch = rest[-6:]
    running_kernel(blocks, lambda k, r: lines[k][pl.ds(r, 1)], out_ref, *scratch)


def running_call(body, specs, args, n, rows, days, width, plane):
    cell = width // plane
    return pl.pallas_call(
        body,
        compiler_params=LIMIT,
        in_specs=specs,
        out_specs=IN_HBM,
        out_shape=hbm((plane, n, rows, cell, days)),
        scratch_shapes=[
            pltpu.VMEM((n, rows, days, width), jnp.float32),
            pltpu.VMEM((2, rows, width, PARTS * days), jnp.bfloat16),
            pltpu.VMEM((n, plane, rows, cell, days), jnp.float32),
            pltpu.SemaphoreType.DMA((n,)),
            pltpu.SemaphoreType.DMA((n,)),
        ],
    )(*args)


def running_columns(where, by_row, theirs, ring, steps, plane):
    rows, days, lon = by_row.shape
    body = functools.partial(column_kernel, steps=steps, ring=ring)
    specs = [IN_SMEM, IN_HBM, IN_VMEM]
    args = (where, by_row, theirs)
    return running_call(body, specs, args, len(steps), rows, days, lon // ring, plane)


def running_blocks(blocks, lines, plane):
    n = len(blocks)
    body = functools.partial(block_kernel, n=n)
    specs = [IN_HBM] * n + [IN_VMEM] * n
    return running_call(body, specs, (*blocks, *lines), n, *blocks[0].shape, plane)


def totals_kernel(days_ref, total_ref, days_buf, sems):
    rows, _, lon = days_ref.shape
    cuts = sems.shape[0]
    width = lon // cuts
    copies = [
        pltpu.make_async_copy(
            days_ref.at[:, :, pl.ds(c * width, width)], days_buf.at[:, :, pl.ds(c * width, width)], sems.at[c]
        )
        for c in range(cuts)
    ]
    for copy in copies:
        copy.start()
    for c in range(cuts):
        copies[c].wait()
        for r in range(rows):
            line = jnp.sum(days_buf[r, :, pl.ds(c * width, width)], axis=0, keepdims=True)
            for q in range(total_ref.shape[0]):
                total_ref[q, pl.ds(r, 1), pl.ds(c * width, width)] = line


def block_totals(by_row, copies, cuts=8):
    rows, _, lon = by_row.shape
    return pl.pallas_call(
        totals_kernel,
        compiler_params=LIMIT,
        in_specs=[IN_HBM],
        out_specs=IN_VMEM,
        out_shape=jax.ShapeDtypeStruct((copies, rows, lon), jnp.float32),
        scratch_shapes=[pltpu.VMEM(by_row.shape, jnp.float32), pltpu.SemaphoreType.DMA((cuts,))],
    )(by_row)


def lines_kernel(where_ref, theirs_ref, *line_refs, steps, ring):
    width = theirs_ref.shape[2] // ring
    for step, line_ref in zip(steps, line_refs):
        lanes = pl.ds(pl.multiple_of(ring_place(where_ref, step, ring) * width, width), width)
        line_ref[...] = jnp.zeros_like(line_ref)
        for r in range(theirs_ref.shape[1]):
            line_ref[pl.ds(r, 1)] = carried(theirs_ref, where_ref[1], r, lanes)


def carry_lines(where, theirs, steps, ring):
    width = theirs.shape[2] // ring
    return pl.pallas_call(
        functools.partial(lines_kernel, steps=steps, ring=ring),
        compiler_params=LIMIT,
        in_specs=[IN_SMEM, IN_VMEM],
        out_specs=[IN_VMEM] * len(steps),
        out_shape=[jax.ShapeDtypeStruct((8, width), jnp.float32)] * len(steps),
    )(where, theirs)


def place_kernel(where_ref, piece_ref, *refs):
    refs[-1][...] = piece_ref[...].reshape(refs[-1].shape)


def place(where, whole, ring, piece, steps):
    plane, _, rows, cell, days = piece.shape
    half = plane // 2

    def target(j, h, where):
        step = jnp.int32(steps[0])
        for i, s in enumerate(steps[1:], 1):
            step = jnp.where(j == i, s, step)
        return (lax.rem(where[0] - step + 2 * ring, ring), h, 0, 0, 0)

    args = (where, piece) if whole is None else (where, piece, whole)
    in_specs = [pl.BlockSpec((half, 1, rows, cell, days), lambda j, h, where: (h, j, 0, 0, 0))]
    if whole is not None:
        in_specs.append(pl.BlockSpec(memory_space=pl.ANY))
    return pl.pallas_call(
        place_kernel,
        compiler_params=LIMIT,
        grid_spec=pltpu.PrefetchScalarGridSpec(
            num_scalar_prefetch=1,
            grid=(len(steps), 2),
            in_specs=in_specs,
            out_specs=pl.BlockSpec((1, half, rows, cell, days), target),
        ),
        out_shape=jax.ShapeDtypeStruct((ring, plane, rows, cell, days), jnp.float32),
        input_output_aliases={} if whole is None else {2: 0},
    )(*args)


def place_pair_kernel(where_ref, *refs, steps):
    n = len(steps)
    block_refs, whole_ref, sems = refs[:n], refs[n + 1], refs[n + 2]
    ring = whole_ref.shape[0]
    copies = [
        pltpu.make_async_copy(
            block_refs[k], whole_ref.at[ring_place(where_ref, -step, ring)], sems.at[k]
        )
        for k, step in enumerate(steps)
    ]
    for copy in copies:
        copy.start()
    for copy in copies:
        copy.wait()


def place_blocks(where, whole, blocks, steps):
    n = len(steps)
    blocks = [pltpu.with_memory_space_constraint(block, pltpu.VMEM) for block in blocks]
    return pl.pallas_call(
        functools.partial(place_pair_kernel, steps=steps),
        compiler_params=LIMIT,
        in_specs=[IN_SMEM] + [IN_VMEM] * n + [IN_HBM],
        out_specs=IN_HBM,
        out_shape=jax.ShapeDtypeStruct(whole.shape, jnp.float32),
        scratch_shapes=[pltpu.SemaphoreType.DMA((n,))],
        input_output_aliases={n + 1: 0},
    )(where, *blocks, whole)


def shifted(block, ring, step):
    return lax.ppermute(block, "space_0", [(i, (i + step) % ring) for i in range(ring)])


def exchanged(value, axes):
    return lax.all_to_all(value, axes, split_axis=0, concat_axis=0, tiled=True)


def per_device(precip):
    by_row = jnp.transpose(precip, (1, 0, 2))
    stays = pltpu.with_memory_space_constraint(by_row, pltpu.HBM)
    rows, days, lon = by_row.shape
    ring = lax.axis_size("space_0")
    plane = lax.axis_size("space_1") * lax.axis_size("space_2")
    blocks = lax.axis_size("tm")
    where = jnp.stack([lax.axis_index("space_0"), lax.axis_index("tm")]).astype(jnp.int32)

    def sent(block, step):
        return shifted(block, ring, step)

    def column(step):
        at = lax.rem(where[0] + (step + ring), ring) * (lon // ring)
        return lax.dynamic_slice(by_row, (0, 0, at), (rows, days, lon // ring))

    raw = [sent(column(RING_FIRST[0]), RING_FIRST[0])]
    cut = cut_columns(where, stays, ring, RING_FIRST[1:])
    raw += [sent(cut[k - 1], RING_FIRST[k]) for k in (1, 2)]
    theirs = block_totals(stays, blocks)
    theirs = exchanged(theirs, "tm")
    mixed = running_columns(where, stays, theirs, ring, PLANE_FIRST, plane)
    mixed = exchanged(mixed, PLANE)
    lines = carry_lines(where, theirs, RING_FIRST, ring)
    lines = [sent(line, step) for line, step in zip(lines, RING_FIRST)]
    late = [sent(mixed[:, k], PLANE_FIRST[k]) for k in range(1, len(PLANE_FIRST))]
    second = running_blocks(raw, lines, plane)
    second = exchanged(second, PLANE)
    whole = place(where, None, ring, mixed, (0,))
    whole = place(where, whole, ring, second, RING_FIRST)
    whole = place_blocks(where, whole, late[2:], PLANE_FIRST[3:])
    whole = place_blocks(where, whole, late[:2], PLANE_FIRST[1:3])
    return whole.reshape(ring * plane * rows, lon // (ring * plane), days)


def solution(mesh):
    finer = Mesh(
        mesh.devices.reshape(8, 4, 2, mesh.shape["tm"]), ("space_0", "space_1", "space_2", "tm")
    )
    space = ("space_0", "space_1", "space_2")
    return jax.shard_map(
        per_device,
        mesh=finer,
        in_specs=(P("tm", space, None),),
        out_specs=P(None, space, "tm"),
        check_vma=False,
    )
```

time: 206 us -> 197 us (0.956)
  the two profiles are of different devices: /device:TPU:10 before, /device:TPU:40 now
where the time goes in v2:
time: 197 us
  waiting for transfers between devices  128 us (65%)
  starting transfers between devices  38.2 us (19%)
  Pallas kernels  26 us (13%)
  local copies, waits for them, and re-layouts  4.84 us (2%)
    ppermute x10, waiting for transfers between devices, shifted(): lax.ppermute(block, 'space_0', [(i, (i + step) % ring) for i in range(rin...  106 us
    ppermute x10, starting transfers between devices, shifted(): lax.ppermute(block, 'space_0', [(i, (i + step) % ring) for i in range(rin...  24.1 us
    all_to_all x3, waiting for transfers between devices, exchanged(): return lax.all_to_all(value, axes, split_axis=0, concat_axis=0, tiled=True)  22.1 us
    all_to_all x3, starting transfers between devices, exchanged(): return lax.all_to_all(value, axes, split_axis=0, concat_axis=0, tiled=True)  14 us
    pallas_call x2, Pallas kernels, running_call(): pl.pallas_call(body, compiler_params=LIMIT, in_specs=specs, out_specs=IN_...  8.34 us
    pallas_call x2, Pallas kernels, place(): pl.pallas_call(place_kernel, compiler_params=LIMIT, grid_spec=pltpu.Prefe...  5.6 us
    pallas_call x2, Pallas kernels, place_blocks(): pl.pallas_call(functools.partial(place_pair_kernel, steps=steps), compile...  4.85 us
  transfers between devices with their start and end apart: 13, of which 7 were waited for; matrix products, arithmetic and copies ran while one was open for 2% of the time, Pallas kernels for 7%

profile of v2, /device:TPU:40, one launch (start us, length us, event | category | flops | bytes accessed | tf_op | source)
XLA Modules:
  0.0 196.9 jit_solution(18014890965864527220)
XLA Ops:
  0.0 3.7 %shard_map.17 = f32[4,6,2048]{2,1,0:T(8,128)} custom-call(f32[6,128,2048]{2,1,0:T(8,128)} %bitcast.22), custom_call_target="tpu_custom_call" | custom-call | tf_op jit(solution)/shard_map/pallas_call | solution.py:180
  3.7 4.3 %all-to-all-start = ((f32[4,6,2048]{2,1,0:T(8,128)}), f32[4,6,2048]{2,1,0:T(8,128)S(1)}, u32[]{:S(2)}, u32[]{:S(2)}) async-start(f32[4,6,2048]{2,1,0:T(8,128)} %shard_map.17), calls=%async_computation | async-start | bytes 524288 | tf_op jit(solution)/shard_map/all_to_all | solution.py:277
  8.0 0.1 pad_add_fusion.where_ref
  8.1 6.6 %all-to-all-done.theirs_ref = f32[4,6,2048]{2,1,0:T(8,128)S(1)} async-done(((f32[4,6,2048]{2,1,0:T(8,128)}), f32[4,6,2048]{2,1,0:T(8,128)S(1)}, u32[]{:S(2)}, u32[]{:S(2)}) %all-to-all-start) | async-done | bytes 196640 | tf_op jit(solution)/shard_map/all_to_all | solution.py:277
  14.7 5.5 %shard_map.18 = f32[8,5,6,32,128]{4,3,2,1,0:T(8,128)} custom-call(s32[2]{0:T(128)S(1)} %pad_add_fusion.where_ref, f32[6,128,2048]{2,1,0:T(8,128)} %bitcast.23, f32[4,6,2048]{2,1,0:T(8,128)S(1)} %all-to-all-done.theirs_ref), custom_call_target="tpu_custom_call" | custom-call | tf_op jit(solution)/shard_map/pallas_call | solution.py:127
  20.2 4.9 %all-to-all-start.1 = ((f32[8,5,6,32,128]{4,3,2,1,0:T(8,128)}), f32[8,5,6,32,128]{4,3,2,1,0:T(8,128)}, u32[]{:S(2)}, u32[]{:S(2)}) async-start(f32[8,5,6,32,128]{4,3,2,1,0:T(8,128)} %shard_map.18), calls=%async_computation.1 | async-start | bytes 7864320 | tf_op jit(solution)/shard_map/all_to_all | solution.py:277
  25.1 1.2 dynamic-slice_bitcast_fusion
  26.3 6.4 %collective-permute-start.4 = (f32[6,128,256]{2,1,0:T(8,128)S(1)}, f32[6,128,256]{2,1,0:T(8,128)S(1)}, u32[]{:S(2)}, u32[]{:S(2)}) collective-permute-start(f32[6,128,256]{2,1,0:T(8,128)S(1)} %dynamic-slice_bitcast_fusion), channel_id=1, source_target_pairs={{0,128},{32,160},{64,192},{96,224},{128,0},{160,32},{192,64},{224,... | collective-permute-start | bytes 2359304 | tf_op jit(solution)/shard_map/ppermute | solution.py:273
  32.7 2.9 %shard_map.19 = (f32[6,128,256]{2,1,0:T(8,128)}, f32[6,128,256]{2,1,0:T(8,128)}) custom-call(s32[2]{0:T(128)S(1)} %pad_add_fusion.where_ref, f32[6,128,2048]{2,1,0:T(8,128)} %bitcast.24), custom_call_target="tpu_custom_call" | custom-call | tf_op jit(solution)/shard_map/pallas_call | solution.py:105
  35.6 0.1 collective-permute-start.5
  35.7 5.0 %collective-permute-start.6 = (f32[6,128,256]{2,1,0:T(8,128)}, f32[6,128,256]{2,1,0:T(8,128)S(1)}, u32[]{:S(2)}, u32[]{:S(2)}) collective-permute-start(f32[6,128,256]{2,1,0:T(8,128)} %get-tuple-element.11), channel_id=1, source_target_pairs={{0,160},{32,192},{64,224},{96,0},{128,32},{160,64},{192,96},{224,1... | collective-permute-start | bytes 2359304 | tf_op jit(solution)/shard_map/ppermute | solution.py:273
  40.7 0.6 shard_map.20
  41.3 0.6 collective-permute-start.7
  41.9 4.9 %collective-permute-start.8 = (f32[8,256]{1,0:T(8,128)S(1)}, f32[8,256]{1,0:T(8,128)S(1)}, u32[]{:S(2)}, u32[]{:S(2)}) collective-permute-start(f32[8,256]{1,0:T(8,128)S(1)} %get-tuple-element.13), channel_id=1, source_target_pairs={{0,96},{32,128},{64,160},{96,192},{128,224},{160,0},{192,32},{224,... | collective-permute-start | bytes 24584 | tf_op jit(solution)/shard_map/ppermute | solution.py:273
  46.9 71.5 %collective-permute-done.7.refs_3_ = f32[8,256]{1,0:T(8,128)S(1)} collective-permute-done((f32[8,256]{1,0:T(8,128)S(1)}, f32[8,256]{1,0:T(8,128)S(1)}, u32[]{:S(2)}, u32[]{:S(2)}) %collective-permute-start.7) | collective-permute-done | bytes 8224 | tf_op jit(solution)/shard_map/ppermute | solution.py:273
  118.4 0.2 collective-permute-start.9
  118.6 0.1 collective-permute-done.8.refs_4_
  118.7 6.4 %collective-permute-done.9.refs_5_ = f32[8,256]{1,0:T(8,128)S(1)} collective-permute-done((f32[8,256]{1,0:T(8,128)S(1)}, f32[8,256]{1,0:T(8,128)S(1)}, u32[]{:S(2)}, u32[]{:S(2)}) %collective-permute-start.9) | collective-permute-done | bytes 8224 | tf_op jit(solution)/shard_map/ppermute | solution.py:273
  125.1 0.0 collective-permute-done.5.refs_1_
  125.1 2.8 %shard_map.21 = f32[8,3,6,32,128]{4,3,2,1,0:T(8,128)} custom-call(f32[6,128,256]{2,1,0:T(8,128)S(1)} %collective-permute-done.4.refs_0_, f32[6,128,256]{2,1,0:T(8,128)S(1)} %collective-permute-done.5.refs_1_, f32[6,128,256]{2,1,0:T(8,128)S(1)} %collective-permute-done.6.refs_2_, f32[8,256]{1,0:T(8,128)S(1)} %collective-permute-done.7.refs_3_, ...), custom_call_target="tpu_custom_call" | custom-call | tf_op jit(solution)/shard_map/pallas_call | solution.py:127
  127.9 4.8 %all-to-all-start.2 = ((f32[8,3,6,32,128]{4,3,2,1,0:T(8,128)}), f32[8,3,6,32,128]{4,3,2,1,0:T(8,128)S(1)}, u32[]{:S(2)}, u32[]{:S(2)}) async-start(f32[8,3,6,32,128]{4,3,2,1,0:T(8,128)} %shard_map.21), calls=%async_computation.2 | async-start | bytes 4718592 | tf_op jit(solution)/shard_map/all_to_all | solution.py:277
  132.8 3.6 %slice_bitcast_fusion = (f32[8,6,32,128]{3,2,1,0:T(8,128)}, f32[8,6,32,128]{3,2,1,0:T(8,128)}, f32[8,6,32,128]{3,2,1,0:T(8,128)}, f32[8,6,32,128]{3,2,1,0:T(8,128)}) fusion(f32[8,5,6,32,128]{4,3,2,1,0:T(8,128)} %all-to-all-done.1.piece_ref), kind=kLoop, calls=%fused_computation | loop fusion | bytes 6291456 | tf_op jit(solution)/shard_map/squeeze | solution.py:305
  136.4 1.0 collective-permute-start.3
  137.4 1.0 collective-permute-start.2
  138.4 4.9 %collective-permute-start.1 = (f32[8,6,32,128]{3,2,1,0:T(8,128)}, f32[8,6,32,128]{3,2,1,0:T(8,128)S(1)}, u32[]{:S(2)}, u32[]{:S(2)}) collective-permute-start(f32[8,6,32,128]{3,2,1,0:T(8,128)} %get-tuple-element.17), channel_id=1, source_target_pairs={{0,192},{32,224},{64,0},{96,32},{128,64},{160,96},{192,128},{224,1... | collective-permute-start | bytes 2359304 | tf_op jit(solution)/shard_map/ppermute | solution.py:273
  143.3 2.5 %shard_map.22.refs_0_ = f32[8,8,6,32,128]{4,3,2,1,0:T(8,128)} custom-call(s32[2]{0:T(128)S(1)} %pad_add_fusion.where_ref, f32[8,5,6,32,128]{4,3,2,1,0:T(8,128)} %all-to-all-done.1.piece_ref), custom_call_target="tpu_custom_call" | custom-call | tf_op jit(solution)/shard_map/pallas_call | solution.py:228
  145.8 15.5 %all-to-all-done.2.piece_ref = f32[8,3,6,32,128]{4,3,2,1,0:T(8,128)S(1)} async-done(((f32[8,3,6,32,128]{4,3,2,1,0:T(8,128)}), f32[8,3,6,32,128]{4,3,2,1,0:T(8,128)S(1)}, u32[]{:S(2)}, u32[]{:S(2)}) %all-to-all-start.2) | async-done | bytes 2359328 | tf_op jit(solution)/shard_map/all_to_all | solution.py:277
  161.3 3.1 %shard_map.23.refs_2_ = f32[8,8,6,32,128]{4,3,2,1,0:T(8,128)} custom-call(s32[2]{0:T(128)S(1)} %pad_add_fusion.where_ref, f32[8,3,6,32,128]{4,3,2,1,0:T(8,128)S(1)} %all-to-all-done.2.piece_ref, f32[8,8,6,32,128]{4,3,2,1,0:T(8,128)} %shard_map.22.refs_0_), custom_call_target="tpu_custom_call", output_to_operand_aliasing={{}: (2, {})} | custom-call | tf_op jit(solution)/shard_map/pallas_call | solution.py:228
  164.4 2.5 %shard_map.24.refs_2_ = f32[8,8,6,32,128]{4,3,2,1,0:T(8,128)} custom-call(s32[2]{0:T(128)S(1)} %pad_add_fusion.where_ref, f32[8,6,32,128]{3,2,1,0:T(8,128)} %collective-permute-done.2.refs_0_, f32[8,6,32,128]{3,2,1,0:T(8,128)} %collective-permute-done.3.refs_1_, f32[8,8,6,32,128]{4,3,2,1,0:T(8,128)} %shard_map.23.refs_2_), custom_call_target="tpu_custom_call", output_to_operand_aliasing={{}: (3, {})} | custom-call | tf_op jit(solution)/shard_map/pallas_call | solution.py:261
  167.0 9.9 %collective-permute-done.1.refs_1_ = f32[8,6,32,128]{3,2,1,0:T(8,128)S(1)} collective-permute-done((f32[8,6,32,128]{3,2,1,0:T(8,128)}, f32[8,6,32,128]{3,2,1,0:T(8,128)S(1)}, u32[]{:S(2)}, u32[]{:S(2)}) %collective-permute-start.1) | collective-permute-done | bytes 786464 | tf_op jit(solution)/shard_map/ppermute | solution.py:273
  176.9 17.7 %collective-permute-done.refs_0_ = f32[8,6,32,128]{3,2,1,0:T(8,128)} collective-permute-done((f32[8,6,32,128]{3,2,1,0:T(8,128)}, f32[8,6,32,128]{3,2,1,0:T(8,128)}, u32[]{:S(2)}, u32[]{:S(2)}) %collective-permute-start) | collective-permute-done | bytes 786464 | tf_op jit(solution)/shard_map/ppermute | solution.py:273
  194.6 2.3 %shard_map.25 = f32[8,8,6,32,128]{4,3,2,1,0:T(8,128)} custom-call(s32[2]{0:T(128)S(1)} %pad_add_fusion.where_ref, f32[8,6,32,128]{3,2,1,0:T(8,128)} %collective-permute-done.refs_0_, f32[8,6,32,128]{3,2,1,0:T(8,128)S(1)} %collective-permute-done.1.refs_1_, f32[8,8,6,32,128]{4,3,2,1,0:T(8,128)} %shard_map.24.refs_2_), custom_call_target="tpu_custom_call", output_to_operand_aliasing={{}: (3, {})} | custom-call | tf_op jit(solution)/shard_map/pallas_call | solution.py:261
  (6 shorter events, 0.0 us)
Async XLA Ops:
  3.7 11.0 %all-to-all-start = ((f32[4,6,2048]{2,1,0:T(8,128)}), f32[4,6,2048]{2,1,0:T(8,128)S(1)}, u32[]{:S(2)}, u32[]{:S(2)}) async-start(f32[4,6,2048]{2,1,0:T(8,128)} %shard_map.17), calls=%async_computation | async-start | bytes 524288 | tf_op jit(solution)/shard_map/all_to_all | solution.py:277
  20.2 107.8 %all-to-all-start.1 = ((f32[8,5,6,32,128]{4,3,2,1,0:T(8,128)}), f32[8,5,6,32,128]{4,3,2,1,0:T(8,128)}, u32[]{:S(2)}, u32[]{:S(2)}) async-start(f32[8,5,6,32,128]{4,3,2,1,0:T(8,128)} %shard_map.18), calls=%async_computation.1 | async-start | bytes 7864320 | tf_op jit(solution)/shard_map/all_to_all | solution.py:277
  26.3 98.8 %collective-permute-start.4 = (f32[6,128,256]{2,1,0:T(8,128)S(1)}, f32[6,128,256]{2,1,0:T(8,128)S(1)}, u32[]{:S(2)}, u32[]{:S(2)}) collective-permute-start(f32[6,128,256]{2,1,0:T(8,128)S(1)} %dynamic-slice_bitcast_fusion), channel_id=1, source_target_pairs={{0,128},{32,160},{64,192},{96,224},{128,0},{160,32},{192,64},{224,... | collective-permute-start | bytes 2359304 | tf_op jit(solution)/shard_map/ppermute | solution.py:273
  35.6 89.5 %collective-permute-start.5 = (f32[6,128,256]{2,1,0:T(8,128)}, f32[6,128,256]{2,1,0:T(8,128)S(1)}, u32[]{:S(2)}, u32[]{:S(2)}) collective-permute-start(f32[6,128,256]{2,1,0:T(8,128)} %get-tuple-element.10), channel_id=1, source_target_pairs={{0,96},{32,128},{64,160},{96,192},{128,224},{160,0},{192,32},{224,... | collective-permute-start | bytes 2359304 | tf_op jit(solution)/shard_map/ppermute | solution.py:273
  35.7 89.4 %collective-permute-start.6 = (f32[6,128,256]{2,1,0:T(8,128)}, f32[6,128,256]{2,1,0:T(8,128)S(1)}, u32[]{:S(2)}, u32[]{:S(2)}) collective-permute-start(f32[6,128,256]{2,1,0:T(8,128)} %get-tuple-element.11), channel_id=1, source_target_pairs={{0,160},{32,192},{64,224},{96,0},{128,32},{160,64},{192,96},{224,1... | collective-permute-start | bytes 2359304 | tf_op jit(solution)/shard_map/ppermute | solution.py:273
  41.3 77.1 %collective-permute-start.7 = (f32[8,256]{1,0:T(8,128)S(1)}, f32[8,256]{1,0:T(8,128)S(1)}, u32[]{:S(2)}, u32[]{:S(2)}) collective-permute-start(f32[8,256]{1,0:T(8,128)S(1)} %get-tuple-element.12), channel_id=1, source_target_pairs={{0,128},{32,160},{64,192},{96,224},{128,0},{160,32},{192,64},{224,... | collective-permute-start | bytes 24584 | tf_op jit(solution)/shard_map/ppermute | solution.py:273
  41.9 76.8 %collective-permute-start.8 = (f32[8,256]{1,0:T(8,128)S(1)}, f32[8,256]{1,0:T(8,128)S(1)}, u32[]{:S(2)}, u32[]{:S(2)}) collective-permute-start(f32[8,256]{1,0:T(8,128)S(1)} %get-tuple-element.13), channel_id=1, source_target_pairs={{0,96},{32,128},{64,160},{96,192},{128,224},{160,0},{192,32},{224,... | collective-permute-start | bytes 24584 | tf_op jit(solution)/shard_map/ppermute | solution.py:273
  118.4 6.7 %collective-permute-start.9 = (f32[8,256]{1,0:T(8,128)S(1)}, f32[8,256]{1,0:T(8,128)S(1)}, u32[]{:S(2)}, u32[]{:S(2)}) collective-permute-start(f32[8,256]{1,0:T(8,128)S(1)} %get-tuple-element.14), channel_id=1, source_target_pairs={{0,160},{32,192},{64,224},{96,0},{128,32},{160,64},{192,96},{224,1... | collective-permute-start | bytes 24584 | tf_op jit(solution)/shard_map/ppermute | solution.py:273
  127.9 33.3 %all-to-all-start.2 = ((f32[8,3,6,32,128]{4,3,2,1,0:T(8,128)}), f32[8,3,6,32,128]{4,3,2,1,0:T(8,128)S(1)}, u32[]{:S(2)}, u32[]{:S(2)}) async-start(f32[8,3,6,32,128]{4,3,2,1,0:T(8,128)} %shard_map.21), calls=%async_computation.2 | async-start | bytes 4718592 | tf_op jit(solution)/shard_map/all_to_all | solution.py:277
  136.4 28.0 %collective-permute-start.3 = (f32[8,6,32,128]{3,2,1,0:T(8,128)}, f32[8,6,32,128]{3,2,1,0:T(8,128)}, u32[]{:S(2)}, u32[]{:S(2)}) collective-permute-start(f32[8,6,32,128]{3,2,1,0:T(8,128)} %get-tuple-element.15), channel_id=1, source_target_pairs={{0,224},{32,0},{64,32},{96,64},{128,96},{160,128},{192,160},{224,1... | collective-permute-start | bytes 2359304 | tf_op jit(solution)/shard_map/ppermute | solution.py:273
  137.4 27.1 %collective-permute-start.2 = (f32[8,6,32,128]{3,2,1,0:T(8,128)}, f32[8,6,32,128]{3,2,1,0:T(8,128)}, u32[]{:S(2)}, u32[]{:S(2)}) collective-permute-start(f32[8,6,32,128]{3,2,1,0:T(8,128)} %get-tuple-element.16), channel_id=1, source_target_pairs={{0,32},{32,64},{64,96},{96,128},{128,160},{160,192},{192,224},{224... | collective-permute-start | bytes 2359304 | tf_op jit(solution)/shard_map/ppermute | solution.py:273
  138.4 38.5 %collective-permute-start.1 = (f32[8,6,32,128]{3,2,1,0:T(8,128)}, f32[8,6,32,128]{3,2,1,0:T(8,128)S(1)}, u32[]{:S(2)}, u32[]{:S(2)}) collective-permute-start(f32[8,6,32,128]{3,2,1,0:T(8,128)} %get-tuple-element.17), channel_id=1, source_target_pairs={{0,192},{32,224},{64,0},{96,32},{128,64},{160,96},{192,128},{224,1... | collective-permute-start | bytes 2359304 | tf_op jit(solution)/shard_map/ppermute | solution.py:273
  143.3 51.3 %collective-permute-start = (f32[8,6,32,128]{3,2,1,0:T(8,128)}, f32[8,6,32,128]{3,2,1,0:T(8,128)}, u32[]{:S(2)}, u32[]{:S(2)}) collective-permute-start(f32[8,6,32,128]{3,2,1,0:T(8,128)} %get-tuple-element.18), channel_id=1, source_target_pairs={{0,64},{32,96},{64,128},{96,160},{128,192},{160,224},{192,0},{224,... | collective-permute-start | bytes 2359304 | tf_op jit(solution)/shard_map/ppermute | solution.py:273
